TPU v7x, 1024 devices: a whole 4x4x32 slice. The times are simulated.
1024 devices in a mesh: head: 8 (over x, z_hi), outer: 4 (over y), inner: 32 (over z_lo, core).
Axes of the slice: x: 4, y: 4, z: 32 (z_hi: 2, z_lo: 16; z = z_hi * 16 + z_lo), core: 2. Of those that a mesh axis runs over, the one named last changes fastest.
Arguments:
- queries: bfloat16 [128, 256, 4096], P(('outer', 'inner'), 'head'), may hold values from -120 to 120
- keys: bfloat16 [128, 256, 1024], P(('outer', 'inner'), 'head'), may hold values from -6 to 6
- values: bfloat16 [128, 256, 1024], P(('outer', 'inner'), 'head'), may hold values from -6 to 6
- doc_lengths: int32 [16], replicated, may hold values from 1 to 4096, 32768 in all
Outputs:
- attended: bfloat16 [128, 256, 4096], P(('outer', 'inner'), 'head')
Inputs may be any that keep to these rules, and one draw needn't show every extreme that they name: `doc_lengths`: the documents of the packed sequence in order, summing to 32768.
All inputs are finite; a program needn't handle non-finite values.
Results may differ from a plain program's by a relative error of at most 0.0044.
Values may be sent and summed in bfloat16 or wider, within the bound.
No kernel may reach another device: no remote copies, remote signals or barrier semaphores. Data moves between devices by JAX's collectives and lax.ppermute only.
A program may use at most 32 MiB of HBM per device.

v0:
```python
import functools
import math

import jax
import jax.numpy as jnp
from jax import lax
from jax.experimental import pallas as pl
from jax.experimental.pallas import tpu as pltpu
from jax.sharding import Mesh
from jax.sharding import PartitionSpec as P


HD = 128
ROWS = 32
HEADS = 4
CHUNK = 64
NEG_FILL = -1e30
AXES = ("x", "zh", "y", "zl", "c")
PLANE = ("x", "c")
RING = ("zh", "y", "zl")

STEPS = (
    ("m1", (0,), (-9,), -9),
    ("p1", (0,), (3,), 3),
    ("p2", (3,), (6,), 3),
    ("e1", (0, 3), (1, 4), 1),
    ("m2", (-9,), (-12,), -3),
    ("e2", (6, -9), (7, -8), 1),
    ("m3", (-12,), (-15,), -3),
    ("g2", (1, 4, 7, -12), (2, 5, 8, -11), 1),
    ("g1", (-9, -12), (-10, -13), -1),
    ("h2", (-15,), (-14,), 1),
    ("h1", (-15,), (-16,), -1),
)
CALLS = (
    (0, 3, 6, 1, 4, -9),
    (7, -8, -12, 2, 5, 8, -10, -11, -13, -15),
    (-14, -16),
)


class Plan:
    def __init__(self, outer, half, halves):
        length, chips = half * halves, outer * half
        index = lambda z, y: ((z // half) * outer + y) * half + z % half
        where = {(z, y * half + z % half): index(z, y) for z in range(length) for y in range(outer)}
        held = {0: {key: key for key in where}}
        moves = {}
        for name, sent, got, shift in STEPS:
            target = {}
            for slot, new in zip(sent, got):
                held[new] = {}
                for (z, n), (zs, ns) in held[slot].items():
                    z2 = (z + shift) % length
                    to = (z2, (ns + (z2 - zs) % half) % chips)
                    assert target.setdefault((z, n), to) == to
                    held[new][to] = (zs, ns)
            assert len(set(target.values())) == len(target)
            moves[name] = target
        wanted = {s: {key for key in where if at[key][1] <= key[1]} for s, at in held.items()}
        self.pairs = {}
        for name, sent, got, shift in reversed(STEPS):
            used = {a: b for a, b in moves[name].items() if any(b in wanted[s] for s in got)}
            for slot, new in zip(sent, got):
                wanted[slot] |= {a for a, b in used.items() if b in wanted[new]}
            self.pairs[name] = [(where[a], where[b]) for a, b in sorted(used.items())]
        for (z, n) in where:
            want = {(h * half + m % half, m) for m in range(max(0, n - half // 2), n + 1) for h in range(halves)}
            got = [held[s][z, n] for call in CALLS for s in call]
            assert len(set(got)) == len(got) and want <= set(got)


def row_offsets(shape, dim):
    i = lax.broadcasted_iota(jnp.int32, shape, dim)
    return ((i >> 5) & 1) * 256 + (i >> 6) * 64 + (i & 31)


def document_bounds(lengths):
    count = lengths.shape[0]
    lane = lax.broadcasted_iota(jnp.int32, (1, HD), 1)
    begin = jnp.where(lane == count, -(1 << 24), 1 << 24)
    end = jnp.where(lane == count, 0, -(1 << 24))
    at = jnp.int32(0)
    for d in range(count):
        begin = jnp.where(lane == d, at, begin)
        at = at + lengths[d]
        end = jnp.where(lane == d, at, end)
    return begin, end


def attend_kernel(slots, first, last, *refs):
    count = len(slots)
    refs = list(refs)
    arrays = max(a for _, a, _ in slots) + 1
    if first:
        lengths, q_ref, *refs = refs
    else:
        bounds, q_all, top_in, acc_in, *refs = refs
    kv, refs = refs[:arrays], refs[arrays:]
    if last:
        out_ref, tops, *refs = refs
    elif first:
        bounds, q_all, tops, acc_out, *refs = refs
    else:
        tops, acc_out, *refs = refs
    k_all, v_all, *refs = refs
    scores, rounded = refs[:2], refs[2:]
    unit = math.log2(math.e) / math.sqrt(HD)
    half, halves = lax.axis_size("zl"), lax.axis_size("zh")

    chip = lax.axis_index("y") * half + lax.axis_index("zl")
    zh = lax.axis_index("zh")
    offsets = row_offsets((256, HD), 0)

    def members(base):
        return (offsets >= bounds[0:1] - base) & (offsets < bounds[1:2] - base)

    if first:
        begin, end = document_bounds(lengths)
        bounds[0:1], bounds[1:2] = begin, end
        apart = jnp.where(members(chip * 512 + zh * ROWS), 0.0, NEG_FILL).astype(jnp.bfloat16)
        for h in range(HEADS):
            q_all[h, :, :HD] = q_ref[:, h].reshape(256, HD)
            q_all[h, :, HD:] = apart

    def run():
        later = {}
        for j, (slot, a, i) in enumerate(slots):
            rows = slice(j * 256, (j + 1) * 256)
            back = slot if slot >= 0 else slot + half
            from_zh = ((zh * half + lax.axis_index("zl") - slot + half * halves) >> 4) & 1
            base = (chip - back) * 512 + from_zh * ROWS
            k_all[rows, :HD] = kv[a][i, :, 0].reshape(256, HD)
            k_all[rows, HD:] = jnp.where(members(base), 1.0, 0.0).astype(jnp.bfloat16)
            v_all[rows, :HD] = kv[a][i, :, 1].reshape(256, HD)
            if back == 0:
                later[j] = (from_zh - zh) * ROWS
        v_all[:, HD:] = jnp.ones((count * 256, HD), jnp.bfloat16)

        def score(h):
            scores[h & 1][...] = lax.dot_general(
                q_all[h], k_all[...], (((1,), (1,)), ((), ())), preferred_element_type=jnp.float32
            )

        def weigh(h):
            for r in range(0, 256, CHUNK):
                rows = slice(r, r + CHUNK)
                wide = None
                for j in range(count):
                    cols = slice(j * 256, (j + 1) * 256)
                    s = scores[h & 1][rows, cols]
                    if j in later:
                        q_at = row_offsets((256, 1), 0)[rows] - later[j]
                        s = jnp.where(row_offsets((1, 256), 1) <= q_at, s, NEG_FILL)
                        scores[h & 1][rows, cols] = s
                    wide = s if wide is None else jnp.maximum(wide, s)
                top = jnp.max(wide, axis=1, keepdims=True)
                if not first:
                    top = jnp.maximum(top_in[h, rows], top)
                for j in range(count):
                    cols = slice(j * 256, (j + 1) * 256)
                    w = jnp.exp2((scores[h & 1][rows, cols] - top) * unit)
                    rounded[h & 1][rows, cols] = w.astype(jnp.bfloat16)
                tops[h, rows] = top

        def gather(h):
            for r in range(0, 256, 128):
                rows = slice(r, r + 128)
                added = jnp.dot(rounded[h & 1][rows], v_all[...], preferred_element_type=jnp.float32)
                if not first:
                    factor = jnp.exp2((top_in[h, rows] - tops[h, rows]) * unit)
                    added = added + acc_in[h, rows] * factor
                if last:
                    res = added[:, :HD] / added[:, HD:]
                    out_ref[r // ROWS : r // ROWS + 4, h] = res.astype(jnp.bfloat16).reshape(4, ROWS, HD)
                else:
                    acc_out[h, rows] = added

        for h in range(HEADS + 2):
            if h < HEADS:
                score(h)
            if h >= 2:
                gather(h - 2)
            if 1 <= h <= HEADS:
                weigh(h - 1)

    nearest = min(s if s >= 0 else s + half for s, _, _ in slots)
    if first or last or nearest == 0:
        run()
        return
    pl.when(chip >= nearest)(run)

    @pl.when(chip < nearest)
    def _():
        tops[...] = top_in[...]
        acc_out[...] = acc_in[...]


VMEM = pl.BlockSpec(memory_space=pltpu.VMEM)
SMEM = pl.BlockSpec(memory_space=pltpu.SMEM)


def attend(heads_in, slots, blocks, state, last):
    n = len(blocks)
    first = state is None
    bounds = jax.ShapeDtypeStruct((8, HD), jnp.int32)
    q_all = jax.ShapeDtypeStruct((HEADS, 256, 2 * HD), jnp.bfloat16)
    top = jax.ShapeDtypeStruct((HEADS, 256, 1), jnp.float32)
    acc = jax.ShapeDtypeStruct((HEADS, 256, 2 * HD), jnp.float32)
    out = jax.ShapeDtypeStruct((8, HEADS, ROWS, HD), jnp.bfloat16)
    outs = out if last else (bounds, q_all, top, acc) if first else (top, acc)
    arrays = list({id(b): b for b, _ in blocks}.values())
    number = {id(b): a for a, b in enumerate(arrays)}
    where = tuple((s, number[id(b)], i) for s, (b, i) in zip(slots, blocks))
    return pl.pallas_call(
        functools.partial(attend_kernel, where, first, last),
        out_shape=outs,
        in_specs=([SMEM, VMEM] if first else [VMEM] * 4) + [VMEM] * len(arrays),
        out_specs=VMEM if last else tuple(VMEM for _ in outs),
        scratch_shapes=([pltpu.VMEM(top.shape, top.dtype)] if last else [])
        + [
            pltpu.VMEM((n * 256, 2 * HD), jnp.bfloat16),
            pltpu.VMEM((n * 256, 2 * HD), jnp.bfloat16),
            pltpu.VMEM((256, n * 256), jnp.float32),
            pltpu.VMEM((256, n * 256), jnp.float32),
            pltpu.VMEM((256, n * 256), jnp.bfloat16),
            pltpu.VMEM((256, n * 256), jnp.bfloat16),
        ],
        compiler_params=pltpu.CompilerParams(vmem_limit_bytes=(6 + 2 * n) << 20),
        cost_estimate=pl.CostEstimate(
            flops=n * HEADS * 256 * 256 * HD * 4,
            bytes_accessed=n * 131072 + 1500000,
            transcendentals=n * HEADS * 256 * 256,
        ),
    )(*heads_in, *(() if first else state), *arrays)


def copy_all(copies):
    for c in copies:
        c.start()
    for c in copies:
        c.wait()


def pack_kv_kernel(k_ref, v_ref, out_ref, sems):
    copy_all(
        [
            pltpu.make_async_copy(
                ref.at[0, :, g * HD : (g + 1) * HD], out_ref.at[g, part], sems.at[2 * g + part]
            )
            for g in range(8)
            for part, ref in enumerate((k_ref, v_ref))
        ]
    )


def pack_q_kernel(q_ref, out_ref, sems):
    copy_all(
        [
            pltpu.make_async_copy(
                q_ref.at[0, :, i * HD : (i + 1) * HD],
                out_ref.at[i // HEADS, i % HEADS],
                sems.at[i],
            )
            for i in range(8 * HEADS)
        ]
    )


def unpack_kernel(in_ref, out_ref, sems):
    copy_all(
        [
            pltpu.make_async_copy(
                in_ref.at[i // HEADS, i % HEADS],
                out_ref.at[0, :, i * HD : (i + 1) * HD],
                sems.at[i],
            )
            for i in range(8 * HEADS)
        ]
    )


def unpack(array):
    return pl.pallas_call(
        unpack_kernel,
        out_shape=jax.ShapeDtypeStruct((1, ROWS, 8 * HEADS * HD), jnp.bfloat16),
        in_specs=[VMEM],
        out_specs=pl.BlockSpec(memory_space=pltpu.HBM),
        scratch_shapes=[pltpu.SemaphoreType.DMA((8 * HEADS,))],
        compiler_params=pltpu.CompilerParams(vmem_limit_bytes=4 << 20),
    )(array)


def pack(kernel, shape, *arrays):
    return pl.pallas_call(
        kernel,
        out_shape=jax.ShapeDtypeStruct(shape, jnp.bfloat16),
        in_specs=[pl.BlockSpec(memory_space=pltpu.HBM)] * len(arrays),
        out_specs=VMEM,
        scratch_shapes=[pltpu.SemaphoreType.DMA((shape[0] * shape[1],))],
        compiler_params=pltpu.CompilerParams(vmem_limit_bytes=4 << 20),
    )(*[pltpu.with_memory_space_constraint(a, pltpu.HBM) for a in arrays])


def body(plan, *args):
    return spread(plan, *args)


def spread(plan, queries, keys, values, doc_lengths):
    kv = pack(pack_kv_kernel, (8, 2, ROWS, HD), keys, values)
    own = lax.all_to_all(kv, PLANE, split_axis=0, concat_axis=0, tiled=True)
    q = pack(pack_q_kernel, (8, HEADS, ROWS, HD), queries)
    q = lax.all_to_all(q, PLANE, split_axis=0, concat_axis=0, tiled=True)

    held = {0: (own[None], 0)}
    for name, sent, got, _ in STEPS:
        parts = [held[s][0][held[s][1]] for s in sent]
        if len(parts) > 1:
            parts = lax.optimization_barrier(parts)
        back = lax.ppermute(jnp.stack(parts), RING, plan.pairs[name])
        for i, s in enumerate(got):
            held[s] = (back, i)

    heads_in, state = (doc_lengths, q), None
    for j, call in enumerate(CALLS):
        state = attend(heads_in, call, [held[s] for s in call], state, j == len(CALLS) - 1)
        if j == 0:
            heads_in, state = state[:2], state[2:]
    out = lax.all_to_all(state, PLANE, split_axis=0, concat_axis=0, tiled=True)
    return unpack(out)


def solution(mesh):
    fine = Mesh(mesh.devices.reshape(4, 2, 4, 16, 2), AXES)
    spec = P(("y", "zl", "c"), ("x", "zh"), None)
    return jax.shard_map(
        functools.partial(body, Plan(4, 16, 2)),
        mesh=fine,
        in_specs=(spec, spec, spec, P()),
        out_specs=spec,
        check_vma=False,
    )
```

profile of v0, /device:TPU:56, one launch (start us, length us, event | category | flops | bytes accessed | tf_op | source)
XLA Modules:
  0.0 139.0 jit_solution(17054803898751376185)
XLA Ops:
  0.0 1.0 shard_map.47
  1.0 10.2 %all_to_all.15 = bf16[8,2,32,128]{3,2,1,0:T(8,128)(2,1)S(1)} all-to-all(bf16[8,2,32,128]{3,2,1,0:T(8,128)(2,1)S(1)} %shard_map.47), channel_id=1, replica_groups=mesh['x'=4,'zh'=2,'y'=4,'zl'=16,'c'=2] {'x','c'}, dimensions={0} | all-to-all | bytes 262144 | tf_op jit(solution)/shard_map/all_to_all | solution.py:311
  11.2 7.7 %collective-permute-start = (bf16[1,8,2,32,128]{4,3,2,1,0:T(8,128)(2,1)S(1)}, bf16[1,8,2,32,128]{4,3,2,1,0:T(8,128)(2,1)S(1)}, u32[]{:S(2)}, u32[]{:S(2)}) collective-permute-start(bf16[1,8,2,32,128]{4,3,2,1,0:T(8,128)(2,1)S(1)} %bitcast.21), channel_id=1, source_target_pairs={{0,6},{32,38},{64,70},{96,102},{2,8},{34,40},{66,72},{98,104},{4,1... | collective-permute-start | bytes 393224 | tf_op jit(solution)/shard_map/ppermute | solution.py:320
  18.9 18.6 %collective-permute-start.3 = (bf16[1,8,2,32,128]{4,3,2,1,0:T(8,128)(2,1)S(1)}, bf16[1,8,2,32,128]{4,3,2,1,0:T(8,128)(2,1)S(1)}, u32[]{:S(2)}, u32[]{:S(2)}) collective-permute-start(bf16[1,8,2,32,128]{4,3,2,1,0:T(8,128)(2,1)S(1)} %bitcast.22), channel_id=1, source_target_pairs={{0,142},{32,174},{64,206},{96,238},{2,144},{34,176},{66,208},{98,2... | collective-permute-start | bytes 393224 | tf_op jit(solution)/shard_map/ppermute | solution.py:320
  37.6 2.0 %collective-permute-done.refs_3_ = bf16[1,8,2,32,128]{4,3,2,1,0:T(8,128)(2,1)S(1)} collective-permute-done((bf16[1,8,2,32,128]{4,3,2,1,0:T(8,128)(2,1)S(1)}, bf16[1,8,2,32,128]{4,3,2,1,0:T(8,128)(2,1)S(1)}, u32[]{:S(2)}, u32[]{:S(2)}) %collective-permute-start) | collective-permute-done | bytes 131104 | tf_op jit(solution)/shard_map/ppermute | solution.py:320
  39.6 3.0 %collective-permute-start.1 = (bf16[1,8,2,32,128]{4,3,2,1,0:T(8,128)(2,1)S(1)}, bf16[1,8,2,32,128]{4,3,2,1,0:T(8,128)(2,1)S(1)}, u32[]{:S(2)}, u32[]{:S(2)}) collective-permute-start(bf16[1,8,2,32,128]{4,3,2,1,0:T(8,128)(2,1)S(1)} %collective-permute-done.refs_3_), channel_id=1, source_target_pairs={{32,38},{64,70},{96,102},{34,40},{66,72},{98,104},{36,42},{68,74},... | collective-permute-start | bytes 393224 | tf_op jit(solution)/shard_map/ppermute | solution.py:320
  42.7 1.9 %collective-permute-start.2 = (bf16[2,8,2,32,128]{4,3,2,1,0:T(8,128)(2,1)S(1)}, bf16[2,8,2,32,128]{4,3,2,1,0:T(8,128)(2,1)S(1)}, u32[]{:S(2)}, u32[]{:S(2)}) collective-permute-start(bf16[2,8,2,32,128]{4,3,2,1,0:T(8,128)(2,1)S(1)} %pad_maximum_fusion.1), channel_id=1, source_target_pairs={{0,2},{32,34},{64,66},{96,98},{2,4},{34,36},{66,68},{98,100},{4,6}... | collective-permute-start | bytes 786440 | tf_op jit(solution)/shard_map/ppermute | solution.py:320
  44.6 12.7 %collective-permute-done.3.refs_6_ = bf16[1,8,2,32,128]{4,3,2,1,0:T(8,128)(2,1)S(1)} collective-permute-done((bf16[1,8,2,32,128]{4,3,2,1,0:T(8,128)(2,1)S(1)}, bf16[1,8,2,32,128]{4,3,2,1,0:T(8,128)(2,1)S(1)}, u32[]{:S(2)}, u32[]{:S(2)}) %collective-permute-start.3) | collective-permute-done | bytes 131104 | tf_op jit(solution)/shard_map/ppermute | solution.py:320
  57.3 0.0 collective-permute-done.1.refs_4_
  57.3 2.2 %collective-permute-start.4 = (bf16[2,8,2,32,128]{4,3,2,1,0:T(8,128)(2,1)S(1)}, bf16[2,8,2,32,128]{4,3,2,1,0:T(8,128)(2,1)S(1)}, u32[]{:S(2)}, u32[]{:S(2)}) collective-permute-start(bf16[2,8,2,32,128]{4,3,2,1,0:T(8,128)(2,1)S(1)} %pad_maximum_fusion.2), channel_id=1, source_target_pairs={{32,34},{64,66},{96,98},{34,36},{66,68},{98,100},{36,38},{68,70},{... | collective-permute-start | bytes 786440 | tf_op jit(solution)/shard_map/ppermute | solution.py:320
  59.6 2.0 %collective-permute-start.5 = (bf16[1,8,2,32,128]{4,3,2,1,0:T(8,128)(2,1)S(1)}, bf16[1,8,2,32,128]{4,3,2,1,0:T(8,128)(2,1)S(1)}, u32[]{:S(2)}, u32[]{:S(2)}) collective-permute-start(bf16[1,8,2,32,128]{4,3,2,1,0:T(8,128)(2,1)S(1)} %collective-permute-done.3.refs_6_), channel_id=1, source_target_pairs={{0,250},{32,154},{64,186},{96,218},{2,252},{34,156},{66,188},{98,2... | collective-permute-start | bytes 393224 | tf_op jit(solution)/shard_map/ppermute | solution.py:320
  61.6 0.0 collective-permute-done.2.refs_5_
  61.6 6.5 %collective-permute-done.4.refs_4_ = bf16[2,8,2,32,128]{4,3,2,1,0:T(8,128)(2,1)S(1)} collective-permute-done((bf16[2,8,2,32,128]{4,3,2,1,0:T(8,128)(2,1)S(1)}, bf16[2,8,2,32,128]{4,3,2,1,0:T(8,128)(2,1)S(1)}, u32[]{:S(2)}, u32[]{:S(2)}) %collective-permute-start.4) | collective-permute-done | bytes 262176 | tf_op jit(solution)/shard_map/ppermute | solution.py:320
  68.2 12.3 %collective-permute-done.5.refs_5_ = bf16[1,8,2,32,128]{4,3,2,1,0:T(8,128)(2,1)S(1)} collective-permute-done((bf16[1,8,2,32,128]{4,3,2,1,0:T(8,128)(2,1)S(1)}, bf16[1,8,2,32,128]{4,3,2,1,0:T(8,128)(2,1)S(1)}, u32[]{:S(2)}, u32[]{:S(2)}) %collective-permute-start.5) | collective-permute-done | bytes 131104 | tf_op jit(solution)/shard_map/ppermute | solution.py:320
  80.5 0.1 pad_maximum_fusion
  80.5 1.9 %collective-permute-start.6 = (bf16[4,8,2,32,128]{4,3,2,1,0:T(8,128)(2,1)S(1)}, bf16[4,8,2,32,128]{4,3,2,1,0:T(8,128)(2,1)S(1)}, u32[]{:S(2)}, u32[]{:S(2)}) collective-permute-start(bf16[4,8,2,32,128]{4,3,2,1,0:T(8,128)(2,1)S(1)} %pad_maximum_fusion), channel_id=1, source_target_pairs={{32,34},{64,66},{96,98},{2,4},{34,36},{66,68},{98,100},{4,6},{36,3... | collective-permute-start | bytes 1572872 | tf_op jit(solution)/shard_map/ppermute | solution.py:320
  82.5 1.9 %shard_map.46 = bf16[8,4,32,128]{3,2,1,0:T(8,128)(2,1)} custom-call(bf16[1,32,4096]{2,1,0:T(8,128)(2,1)} %q_ref.1), custom_call_target="tpu_custom_call" | custom-call | tf_op jit(solution)/shard_map/pallas_call | solution.py:295
  84.4 3.4 %all-to-all-start = ((bf16[8,4,32,128]{3,2,1,0:T(8,128)(2,1)}), bf16[8,4,32,128]{3,2,1,0:T(8,128)(2,1)S(1)}, u32[]{:S(2)}, u32[]{:S(2)}) async-start(bf16[8,4,32,128]{3,2,1,0:T(8,128)(2,1)} %shard_map.46), calls=%async_computation | async-start | bytes 524288 | tf_op jit(solution)/shard_map/all_to_all | solution.py:313
  87.8 0.0 copy-start
  87.9 3.9 %collective-permute-start.7 = (bf16[2,8,2,32,128]{4,3,2,1,0:T(8,128)(2,1)S(1)}, bf16[2,8,2,32,128]{4,3,2,1,0:T(8,128)(2,1)S(1)}, u32[]{:S(2)}, u32[]{:S(2)}) collective-permute-start(bf16[2,8,2,32,128]{4,3,2,1,0:T(8,128)(2,1)S(1)} %pad_maximum_fusion.3), channel_id=1, source_target_pairs={{0,254},{32,158},{64,190},{96,222},{34,32},{66,64},{98,96},{36,34}... | collective-permute-start | bytes 786440 | tf_op jit(solution)/shard_map/ppermute | solution.py:320
  91.8 2.9 %collective-permute-start.8 = (bf16[1,8,2,32,128]{4,3,2,1,0:T(8,128)(2,1)S(1)}, bf16[1,8,2,32,128]{4,3,2,1,0:T(8,128)(2,1)S(1)}, u32[]{:S(2)}, u32[]{:S(2)}) collective-permute-start(bf16[1,8,2,32,128]{4,3,2,1,0:T(8,128)(2,1)S(1)} %collective-permute-done.5.refs_5_), channel_id=1, source_target_pairs={{0,250},{32,154},{64,186},{96,218},{2,252},{34,156},{66,188},{98,2... | collective-permute-start | bytes 393224 | tf_op jit(solution)/shard_map/ppermute | solution.py:320
  94.7 17.5 %collective-permute-done.8.refs_8_ = bf16[1,8,2,32,128]{4,3,2,1,0:T(8,128)(2,1)S(1)} collective-permute-done((bf16[1,8,2,32,128]{4,3,2,1,0:T(8,128)(2,1)S(1)}, bf16[1,8,2,32,128]{4,3,2,1,0:T(8,128)(2,1)S(1)}, u32[]{:S(2)}, u32[]{:S(2)}) %collective-permute-start.8) | collective-permute-done | bytes 131104 | tf_op jit(solution)/shard_map/ppermute | solution.py:320
  112.2 1.9 %collective-permute-start.10 = (bf16[1,8,2,32,128]{4,3,2,1,0:T(8,128)(2,1)S(1)}, bf16[1,8,2,32,128]{4,3,2,1,0:T(8,128)(2,1)S(1)}, u32[]{:S(2)}, u32[]{:S(2)}) collective-permute-start(bf16[1,8,2,32,128]{4,3,2,1,0:T(8,128)(2,1)S(1)} %collective-permute-done.8.refs_8_), channel_id=1, source_target_pairs={{0,254},{32,158},{64,190},{96,222},{2,0},{34,32},{66,64},{98,96},{... | collective-permute-start | bytes 393224 | tf_op jit(solution)/shard_map/ppermute | solution.py:320
  114.1 3.9 %collective-permute-start.9 = (bf16[1,8,2,32,128]{4,3,2,1,0:T(8,128)(2,1)S(1)}, bf16[1,8,2,32,128]{4,3,2,1,0:T(8,128)(2,1)S(1)}, u32[]{:S(2)}, u32[]{:S(2)}) collective-permute-start(bf16[1,8,2,32,128]{4,3,2,1,0:T(8,128)(2,1)S(1)} %collective-permute-done.8.refs_8_), channel_id=1, source_target_pairs={{32,34},{64,66},{96,98},{2,4},{34,36},{66,68},{98,100},{4,6},{36,3... | collective-permute-start | bytes 393224 | tf_op jit(solution)/shard_map/ppermute | solution.py:320
  118.0 0.0 all-to-all-done.refs_1_
  118.0 0.0 copy-done
  118.1 3.0 %shard_map.48 = (s32[8,128]{1,0:T(8,128)S(1)}, bf16[4,256,256]{2,1,0:T(8,128)(2,1)S(1)}, f32[4,256,1]{2,1,0:T(8,128)S(1)}, f32[4,256,256]{2,1,0:T(8,128)S(1)}) custom-call(s32[16]{0:T(128)S(1)} %copy-done, bf16[8,4,32,128]{3,2,1,0:T(8,128)(2,1)S(1)} %all-to-all-done.refs_1_, bf16[1,8,2,32,128]{4,3,2,1,0:T(8,128)(2,1)S(1)} %bitcast.24, ...), custom_call_target="tpu_custom_call" | custom-call | flops 805306368 | bytes 2286432 | tf_op jit(solution)/shard_map/pallas_call | solution.py:215
  121.0 0.0 collective-permute-done.7.refs_7_
  121.0 0.0 collective-permute-done.6.refs_6_
  121.0 3.7 %shard_map.49 = (f32[4,256,1]{2,1,0:T(8,128)S(1)}, f32[4,256,256]{2,1,0:T(8,128)S(1)}) custom-call(s32[8,128]{1,0:T(8,128)S(1)} %get-tuple-element.23.refs_0_, bf16[4,256,256]{2,1,0:T(8,128)(2,1)S(1)} %get-tuple-element.24.refs_1_, f32[4,256,1]{2,1,0:T(8,128)S(1)} %get-tuple-element.25.refs_2_, f32[4,256,256]{2,1,0:T(8,128)S(1)} %get-tuple-element.26.refs_3_, ...), custom_call_target="tpu_custom_call" | custom-call | flops 1342177280 | bytes 2810720 | tf_op jit(solution)/shard_map/pallas_call | solution.py:215
  124.8 0.0 collective-permute-done.10.refs_5_
  124.8 0.0 collective-permute-done.9.refs_4_
  124.8 1.4 shard_map.50
  126.2 11.8 %all_to_all.16.in_ref = bf16[8,4,32,128]{3,2,1,0:T(8,128)(2,1)S(1)} all-to-all(bf16[8,4,32,128]{3,2,1,0:T(8,128)(2,1)S(1)} %shard_map.50), channel_id=1, replica_groups=mesh['x'=4,'zh'=2,'y'=4,'zl'=16,'c'=2] {'x','c'}, dimensions={0} | all-to-all | bytes 524288 | tf_op jit(solution)/shard_map/all_to_all | solution.py:329
  138.0 1.0 shard_map.51
  (5 shorter events, 0.1 us)
Async XLA Ops:
  11.2 28.4 %collective-permute-start = (bf16[1,8,2,32,128]{4,3,2,1,0:T(8,128)(2,1)S(1)}, bf16[1,8,2,32,128]{4,3,2,1,0:T(8,128)(2,1)S(1)}, u32[]{:S(2)}, u32[]{:S(2)}) collective-permute-start(bf16[1,8,2,32,128]{4,3,2,1,0:T(8,128)(2,1)S(1)} %bitcast.21), channel_id=1, source_target_pairs={{0,6},{32,38},{64,70},{96,102},{2,8},{34,40},{66,72},{98,104},{4,1... | collective-permute-start | bytes 393224 | tf_op jit(solution)/shard_map/ppermute | solution.py:320
  18.9 38.4 %collective-permute-start.3 = (bf16[1,8,2,32,128]{4,3,2,1,0:T(8,128)(2,1)S(1)}, bf16[1,8,2,32,128]{4,3,2,1,0:T(8,128)(2,1)S(1)}, u32[]{:S(2)}, u32[]{:S(2)}) collective-permute-start(bf16[1,8,2,32,128]{4,3,2,1,0:T(8,128)(2,1)S(1)} %bitcast.22), channel_id=1, source_target_pairs={{0,142},{32,174},{64,206},{96,238},{2,144},{34,176},{66,208},{98,2... | collective-permute-start | bytes 393224 | tf_op jit(solution)/shard_map/ppermute | solution.py:320
  39.6 17.7 %collective-permute-start.1 = (bf16[1,8,2,32,128]{4,3,2,1,0:T(8,128)(2,1)S(1)}, bf16[1,8,2,32,128]{4,3,2,1,0:T(8,128)(2,1)S(1)}, u32[]{:S(2)}, u32[]{:S(2)}) collective-permute-start(bf16[1,8,2,32,128]{4,3,2,1,0:T(8,128)(2,1)S(1)} %collective-permute-done.refs_3_), channel_id=1, source_target_pairs={{32,38},{64,70},{96,102},{34,40},{66,72},{98,104},{36,42},{68,74},... | collective-permute-start | bytes 393224 | tf_op jit(solution)/shard_map/ppermute | solution.py:320
  42.7 18.9 %collective-permute-start.2 = (bf16[2,8,2,32,128]{4,3,2,1,0:T(8,128)(2,1)S(1)}, bf16[2,8,2,32,128]{4,3,2,1,0:T(8,128)(2,1)S(1)}, u32[]{:S(2)}, u32[]{:S(2)}) collective-permute-start(bf16[2,8,2,32,128]{4,3,2,1,0:T(8,128)(2,1)S(1)} %pad_maximum_fusion.1), channel_id=1, source_target_pairs={{0,2},{32,34},{64,66},{96,98},{2,4},{34,36},{66,68},{98,100},{4,6}... | collective-permute-start | bytes 786440 | tf_op jit(solution)/shard_map/ppermute | solution.py:320
  57.3 10.8 %collective-permute-start.4 = (bf16[2,8,2,32,128]{4,3,2,1,0:T(8,128)(2,1)S(1)}, bf16[2,8,2,32,128]{4,3,2,1,0:T(8,128)(2,1)S(1)}, u32[]{:S(2)}, u32[]{:S(2)}) collective-permute-start(bf16[2,8,2,32,128]{4,3,2,1,0:T(8,128)(2,1)S(1)} %pad_maximum_fusion.2), channel_id=1, source_target_pairs={{32,34},{64,66},{96,98},{34,36},{66,68},{98,100},{36,38},{68,70},{... | collective-permute-start | bytes 786440 | tf_op jit(solution)/shard_map/ppermute | solution.py:320
  59.6 20.9 %collective-permute-start.5 = (bf16[1,8,2,32,128]{4,3,2,1,0:T(8,128)(2,1)S(1)}, bf16[1,8,2,32,128]{4,3,2,1,0:T(8,128)(2,1)S(1)}, u32[]{:S(2)}, u32[]{:S(2)}) collective-permute-start(bf16[1,8,2,32,128]{4,3,2,1,0:T(8,128)(2,1)S(1)} %collective-permute-done.3.refs_6_), channel_id=1, source_target_pairs={{0,250},{32,154},{64,186},{96,218},{2,252},{34,156},{66,188},{98,2... | collective-permute-start | bytes 393224 | tf_op jit(solution)/shard_map/ppermute | solution.py:320
  80.5 40.5 %collective-permute-start.6 = (bf16[4,8,2,32,128]{4,3,2,1,0:T(8,128)(2,1)S(1)}, bf16[4,8,2,32,128]{4,3,2,1,0:T(8,128)(2,1)S(1)}, u32[]{:S(2)}, u32[]{:S(2)}) collective-permute-start(bf16[4,8,2,32,128]{4,3,2,1,0:T(8,128)(2,1)S(1)} %pad_maximum_fusion), channel_id=1, source_target_pairs={{32,34},{64,66},{96,98},{2,4},{34,36},{66,68},{98,100},{4,6},{36,3... | collective-permute-start | bytes 1572872 | tf_op jit(solution)/shard_map/ppermute | solution.py:320
  84.4 33.6 %all-to-all-start = ((bf16[8,4,32,128]{3,2,1,0:T(8,128)(2,1)}), bf16[8,4,32,128]{3,2,1,0:T(8,128)(2,1)S(1)}, u32[]{:S(2)}, u32[]{:S(2)}) async-start(bf16[8,4,32,128]{3,2,1,0:T(8,128)(2,1)} %shard_map.46), calls=%async_computation | async-start | bytes 524288 | tf_op jit(solution)/shard_map/all_to_all | solution.py:313
  87.8 30.2 %copy-start = (s32[16]{0:T(128)S(1)}, s32[16]{0:T(128)}, u32[]{:S(2)}) copy-start(s32[16]{0:T(128)} %refs_0_.1) | copy-start | bytes 196
  87.9 33.2 %collective-permute-start.7 = (bf16[2,8,2,32,128]{4,3,2,1,0:T(8,128)(2,1)S(1)}, bf16[2,8,2,32,128]{4,3,2,1,0:T(8,128)(2,1)S(1)}, u32[]{:S(2)}, u32[]{:S(2)}) collective-permute-start(bf16[2,8,2,32,128]{4,3,2,1,0:T(8,128)(2,1)S(1)} %pad_maximum_fusion.3), channel_id=1, source_target_pairs={{0,254},{32,158},{64,190},{96,222},{34,32},{66,64},{98,96},{36,34}... | collective-permute-start | bytes 786440 | tf_op jit(solution)/shard_map/ppermute | solution.py:320
  91.8 20.4 %collective-permute-start.8 = (bf16[1,8,2,32,128]{4,3,2,1,0:T(8,128)(2,1)S(1)}, bf16[1,8,2,32,128]{4,3,2,1,0:T(8,128)(2,1)S(1)}, u32[]{:S(2)}, u32[]{:S(2)}) collective-permute-start(bf16[1,8,2,32,128]{4,3,2,1,0:T(8,128)(2,1)S(1)} %collective-permute-done.5.refs_5_), channel_id=1, source_target_pairs={{0,250},{32,154},{64,186},{96,218},{2,252},{34,156},{66,188},{98,2... | collective-permute-start | bytes 393224 | tf_op jit(solution)/shard_map/ppermute | solution.py:320
  112.2 12.6 %collective-permute-start.10 = (bf16[1,8,2,32,128]{4,3,2,1,0:T(8,128)(2,1)S(1)}, bf16[1,8,2,32,128]{4,3,2,1,0:T(8,128)(2,1)S(1)}, u32[]{:S(2)}, u32[]{:S(2)}) collective-permute-start(bf16[1,8,2,32,128]{4,3,2,1,0:T(8,128)(2,1)S(1)} %collective-permute-done.8.refs_8_), channel_id=1, source_target_pairs={{0,254},{32,158},{64,190},{96,222},{2,0},{34,32},{66,64},{98,96},{... | collective-permute-start | bytes 393224 | tf_op jit(solution)/shard_map/ppermute | solution.py:320
  114.1 10.7 %collective-permute-start.9 = (bf16[1,8,2,32,128]{4,3,2,1,0:T(8,128)(2,1)S(1)}, bf16[1,8,2,32,128]{4,3,2,1,0:T(8,128)(2,1)S(1)}, u32[]{:S(2)}, u32[]{:S(2)}) collective-permute-start(bf16[1,8,2,32,128]{4,3,2,1,0:T(8,128)(2,1)S(1)} %collective-permute-done.8.refs_8_), channel_id=1, source_target_pairs={{32,34},{64,66},{96,98},{2,4},{34,36},{66,68},{98,100},{4,6},{36,3... | collective-permute-start | bytes 393224 | tf_op jit(solution)/shard_map/ppermute | solution.py:320
where the time goes:
time: 140 us; the launch traced here: 139 us
  starting transfers between devices  53.5 us (38%)
  waiting for transfers between devices  51.1 us (36%)
  blocking collectives  22 us (16%)
  Pallas kernels  12 us (9%)
    ppermute x11, waiting for transfers between devices, spread(): back = lax.ppermute(jnp.stack(parts), RING, plan.pairs[name])  51.1 us
    ppermute x11, starting transfers between devices, spread(): back = lax.ppermute(jnp.stack(parts), RING, plan.pairs[name])  50.1 us
    all_to_all x1, blocking collectives, spread(): out = lax.all_to_all(state, PLANE, split_axis=0, concat_axis=0, tiled=True)  11.8 us
    all_to_all x1, blocking collectives, spread(): own = lax.all_to_all(kv, PLANE, split_axis=0, concat_axis=0, tiled=True)  10.2 us
    pallas_call x3, Pallas kernels, attend(): pl.pallas_call(functools.partial(attend_kernel, where, first, last), out_...  8.1 us
    all_to_all x1, starting transfers between devices, spread(): q = lax.all_to_all(q, PLANE, split_axis=0, concat_axis=0, tiled=True)  3.42 us
    pallas_call x2, Pallas kernels, pack(): pl.pallas_call(kernel, out_shape=jax.ShapeDtypeStruct(shape, jnp.bfloat16...  2.92 us
  transfers between devices with their start and end apart: 12, of which 5 were waited for; matrix products, arithmetic and copies ran while one was open for 0% of the time, Pallas kernels for 6%

commit v1 on v0

--- a/solution.py
+++ b/solution.py
@@ -33,8 +33,10 @@
     ("h1", (-15,), (-16,), -1),
 )
 CALLS = (
-    (0, 3, 6, 1, 4, -9),
-    (7, -8, -12, 2, 5, 8, -10, -11, -13, -15),
+    (0, 3),
+    (6, 1, 4, -9),
+    (7, -8, -12),
+    (2, 5, 8, -10, -11, -13, -15),
     (-14, -16),
 )
 

time: 140 us -> 141 us (level)
  the two profiles are of different devices: /device:TPU:56 before, /device:TPU:8 now
where the time goes in v1:
time: 141 us; the launch traced here: 140 us
  starting transfers between devices  60.3 us (43%)
  waiting for transfers between devices  43.8 us (31%)
  blocking collectives  21.9 us (16%)
  Pallas kernels  13.7 us (10%)
    ppermute x11, starting transfers between devices, spread(): back = lax.ppermute(jnp.stack(parts), RING, plan.pairs[name])  56.9 us
    ppermute x11, waiting for transfers between devices, spread(): back = lax.ppermute(jnp.stack(parts), RING, plan.pairs[name])  43.8 us
    all_to_all x1, blocking collectives, spread(): out = lax.all_to_all(state, PLANE, split_axis=0, concat_axis=0, tiled=True)  11.7 us
    all_to_all x1, blocking collectives, spread(): own = lax.all_to_all(kv, PLANE, split_axis=0, concat_axis=0, tiled=True)  10.2 us
    pallas_call x5, Pallas kernels, attend(): pl.pallas_call(functools.partial(attend_kernel, where, first, last), out_...  9.76 us
    all_to_all x1, starting transfers between devices, spread(): q = lax.all_to_all(q, PLANE, split_axis=0, concat_axis=0, tiled=True)  3.42 us
    pallas_call x2, Pallas kernels, pack(): pl.pallas_call(kernel, out_shape=jax.ShapeDtypeStruct(shape, jnp.bfloat16...  2.92 us
  transfers between devices with their start and end apart: 12, of which 4 were waited for; matrix products, arithmetic and copies ran while one was open for 0% of the time, Pallas kernels for 7%

profile of v1, /device:TPU:8, one launch (start us, length us, event | category | flops | bytes accessed | tf_op | source)
XLA Modules:
  0.0 140.2 jit_solution(14150933372733726603)
XLA Ops:
  0.0 1.0 shard_map.47
  1.0 10.2 %all_to_all.15 = bf16[8,2,32,128]{3,2,1,0:T(8,128)(2,1)S(1)} all-to-all(bf16[8,2,32,128]{3,2,1,0:T(8,128)(2,1)S(1)} %shard_map.47), channel_id=1, replica_groups=mesh['x'=4,'zh'=2,'y'=4,'zl'=16,'c'=2] {'x','c'}, dimensions={0} | all-to-all | bytes 262144 | tf_op jit(solution)/shard_map/all_to_all | solution.py:313
  11.2 6.5 %collective-permute-start = (bf16[1,8,2,32,128]{4,3,2,1,0:T(8,128)(2,1)S(1)}, bf16[1,8,2,32,128]{4,3,2,1,0:T(8,128)(2,1)S(1)}, u32[]{:S(2)}, u32[]{:S(2)}) collective-permute-start(bf16[1,8,2,32,128]{4,3,2,1,0:T(8,128)(2,1)S(1)} %bitcast.21), channel_id=1, source_target_pairs={{0,6},{32,38},{64,70},{96,102},{2,8},{34,40},{66,72},{98,104},{4,1... | collective-permute-start | bytes 393224 | tf_op jit(solution)/shard_map/ppermute | solution.py:322
  17.7 22.0 %collective-permute-start.3 = (bf16[1,8,2,32,128]{4,3,2,1,0:T(8,128)(2,1)S(1)}, bf16[1,8,2,32,128]{4,3,2,1,0:T(8,128)(2,1)S(1)}, u32[]{:S(2)}, u32[]{:S(2)}) collective-permute-start(bf16[1,8,2,32,128]{4,3,2,1,0:T(8,128)(2,1)S(1)} %bitcast.22), channel_id=1, source_target_pairs={{0,142},{32,174},{64,206},{96,238},{2,144},{34,176},{66,208},{98,2... | collective-permute-start | bytes 393224 | tf_op jit(solution)/shard_map/ppermute | solution.py:322
  39.7 0.0 collective-permute-done.refs_3_
  39.7 2.6 %collective-permute-start.1 = (bf16[1,8,2,32,128]{4,3,2,1,0:T(8,128)(2,1)S(1)}, bf16[1,8,2,32,128]{4,3,2,1,0:T(8,128)(2,1)S(1)}, u32[]{:S(2)}, u32[]{:S(2)}) collective-permute-start(bf16[1,8,2,32,128]{4,3,2,1,0:T(8,128)(2,1)S(1)} %collective-permute-done.refs_3_), channel_id=1, source_target_pairs={{32,38},{64,70},{96,102},{34,40},{66,72},{98,104},{36,42},{68,74},... | collective-permute-start | bytes 393224 | tf_op jit(solution)/shard_map/ppermute | solution.py:322
  42.4 4.1 %collective-permute-start.2 = (bf16[2,8,2,32,128]{4,3,2,1,0:T(8,128)(2,1)S(1)}, bf16[2,8,2,32,128]{4,3,2,1,0:T(8,128)(2,1)S(1)}, u32[]{:S(2)}, u32[]{:S(2)}) collective-permute-start(bf16[2,8,2,32,128]{4,3,2,1,0:T(8,128)(2,1)S(1)} %pad_maximum_fusion.1), channel_id=1, source_target_pairs={{0,2},{32,34},{64,66},{96,98},{2,4},{34,36},{66,68},{98,100},{4,6}... | collective-permute-start | bytes 786440 | tf_op jit(solution)/shard_map/ppermute | solution.py:322
  46.5 17.3 %collective-permute-done.3.refs_6_ = bf16[1,8,2,32,128]{4,3,2,1,0:T(8,128)(2,1)S(1)} collective-permute-done((bf16[1,8,2,32,128]{4,3,2,1,0:T(8,128)(2,1)S(1)}, bf16[1,8,2,32,128]{4,3,2,1,0:T(8,128)(2,1)S(1)}, u32[]{:S(2)}, u32[]{:S(2)}) %collective-permute-start.3) | collective-permute-done | bytes 131104 | tf_op jit(solution)/shard_map/ppermute | solution.py:322
  63.8 0.0 collective-permute-done.1.refs_4_
  63.8 1.9 %collective-permute-start.4 = (bf16[2,8,2,32,128]{4,3,2,1,0:T(8,128)(2,1)S(1)}, bf16[2,8,2,32,128]{4,3,2,1,0:T(8,128)(2,1)S(1)}, u32[]{:S(2)}, u32[]{:S(2)}) collective-permute-start(bf16[2,8,2,32,128]{4,3,2,1,0:T(8,128)(2,1)S(1)} %pad_maximum_fusion.2), channel_id=1, source_target_pairs={{32,34},{64,66},{96,98},{34,36},{66,68},{98,100},{36,38},{68,70},{... | collective-permute-start | bytes 786440 | tf_op jit(solution)/shard_map/ppermute | solution.py:322
  65.7 1.9 %collective-permute-start.5 = (bf16[1,8,2,32,128]{4,3,2,1,0:T(8,128)(2,1)S(1)}, bf16[1,8,2,32,128]{4,3,2,1,0:T(8,128)(2,1)S(1)}, u32[]{:S(2)}, u32[]{:S(2)}) collective-permute-start(bf16[1,8,2,32,128]{4,3,2,1,0:T(8,128)(2,1)S(1)} %collective-permute-done.3.refs_6_), channel_id=1, source_target_pairs={{0,250},{32,154},{64,186},{96,218},{2,252},{34,156},{66,188},{98,2... | collective-permute-start | bytes 393224 | tf_op jit(solution)/shard_map/ppermute | solution.py:322
  67.7 0.0 collective-permute-done.2.refs_5_
  67.7 8.2 %collective-permute-done.4.refs_4_ = bf16[2,8,2,32,128]{4,3,2,1,0:T(8,128)(2,1)S(1)} collective-permute-done((bf16[2,8,2,32,128]{4,3,2,1,0:T(8,128)(2,1)S(1)}, bf16[2,8,2,32,128]{4,3,2,1,0:T(8,128)(2,1)S(1)}, u32[]{:S(2)}, u32[]{:S(2)}) %collective-permute-start.4) | collective-permute-done | bytes 262176 | tf_op jit(solution)/shard_map/ppermute | solution.py:322
  75.9 5.0 %collective-permute-done.5.refs_5_ = bf16[1,8,2,32,128]{4,3,2,1,0:T(8,128)(2,1)S(1)} collective-permute-done((bf16[1,8,2,32,128]{4,3,2,1,0:T(8,128)(2,1)S(1)}, bf16[1,8,2,32,128]{4,3,2,1,0:T(8,128)(2,1)S(1)}, u32[]{:S(2)}, u32[]{:S(2)}) %collective-permute-start.5) | collective-permute-done | bytes 131104 | tf_op jit(solution)/shard_map/ppermute | solution.py:322
  80.9 0.1 pad_maximum_fusion
  81.0 1.9 %collective-permute-start.6 = (bf16[4,8,2,32,128]{4,3,2,1,0:T(8,128)(2,1)S(1)}, bf16[4,8,2,32,128]{4,3,2,1,0:T(8,128)(2,1)S(1)}, u32[]{:S(2)}, u32[]{:S(2)}) collective-permute-start(bf16[4,8,2,32,128]{4,3,2,1,0:T(8,128)(2,1)S(1)} %pad_maximum_fusion), channel_id=1, source_target_pairs={{32,34},{64,66},{96,98},{2,4},{34,36},{66,68},{98,100},{4,6},{36,3... | collective-permute-start | bytes 1572872 | tf_op jit(solution)/shard_map/ppermute | solution.py:322
  82.9 1.9 %shard_map.46 = bf16[8,4,32,128]{3,2,1,0:T(8,128)(2,1)} custom-call(bf16[1,32,4096]{2,1,0:T(8,128)(2,1)} %q_ref.1), custom_call_target="tpu_custom_call" | custom-call | tf_op jit(solution)/shard_map/pallas_call | solution.py:297
  84.8 3.4 %all-to-all-start = ((bf16[8,4,32,128]{3,2,1,0:T(8,128)(2,1)}), bf16[8,4,32,128]{3,2,1,0:T(8,128)(2,1)S(1)}, u32[]{:S(2)}, u32[]{:S(2)}) async-start(bf16[8,4,32,128]{3,2,1,0:T(8,128)(2,1)} %shard_map.46), calls=%async_computation | async-start | bytes 524288 | tf_op jit(solution)/shard_map/all_to_all | solution.py:315
  88.3 0.0 copy-start
  88.3 6.0 %collective-permute-start.7 = (bf16[2,8,2,32,128]{4,3,2,1,0:T(8,128)(2,1)S(1)}, bf16[2,8,2,32,128]{4,3,2,1,0:T(8,128)(2,1)S(1)}, u32[]{:S(2)}, u32[]{:S(2)}) collective-permute-start(bf16[2,8,2,32,128]{4,3,2,1,0:T(8,128)(2,1)S(1)} %pad_maximum_fusion.3), channel_id=1, source_target_pairs={{0,254},{32,158},{64,190},{96,222},{34,32},{66,64},{98,96},{36,34}... | collective-permute-start | bytes 786440 | tf_op jit(solution)/shard_map/ppermute | solution.py:322
  94.3 1.9 %collective-permute-start.8 = (bf16[1,8,2,32,128]{4,3,2,1,0:T(8,128)(2,1)S(1)}, bf16[1,8,2,32,128]{4,3,2,1,0:T(8,128)(2,1)S(1)}, u32[]{:S(2)}, u32[]{:S(2)}) collective-permute-start(bf16[1,8,2,32,128]{4,3,2,1,0:T(8,128)(2,1)S(1)} %collective-permute-done.5.refs_5_), channel_id=1, source_target_pairs={{0,250},{32,154},{64,186},{96,218},{2,252},{34,156},{66,188},{98,2... | collective-permute-start | bytes 393224 | tf_op jit(solution)/shard_map/ppermute | solution.py:322
  96.3 0.0 all-to-all-done.refs_1_
  96.3 0.0 copy-done
  96.3 1.6 %shard_map.48 = (s32[8,128]{1,0:T(8,128)S(1)}, bf16[4,256,256]{2,1,0:T(8,128)(2,1)S(1)}, f32[4,256,1]{2,1,0:T(8,128)S(1)}, f32[4,256,256]{2,1,0:T(8,128)S(1)}) custom-call(s32[16]{0:T(128)S(1)} %copy-done, bf16[8,4,32,128]{3,2,1,0:T(8,128)(2,1)S(1)} %all-to-all-done.refs_1_, bf16[1,8,2,32,128]{4,3,2,1,0:T(8,128)(2,1)S(1)} %bitcast.24, ...), custom_call_target="tpu_custom_call" | custom-call | flops 268435456 | bytes 1762144 | tf_op jit(solution)/shard_map/pallas_call | solution.py:217
  97.9 13.3 %collective-permute-done.8.refs_6_ = bf16[1,8,2,32,128]{4,3,2,1,0:T(8,128)(2,1)S(1)} collective-permute-done((bf16[1,8,2,32,128]{4,3,2,1,0:T(8,128)(2,1)S(1)}, bf16[1,8,2,32,128]{4,3,2,1,0:T(8,128)(2,1)S(1)}, u32[]{:S(2)}, u32[]{:S(2)}) %collective-permute-start.8) | collective-permute-done | bytes 131104 | tf_op jit(solution)/shard_map/ppermute | solution.py:322
  111.2 3.7 %collective-permute-start.9 = (bf16[1,8,2,32,128]{4,3,2,1,0:T(8,128)(2,1)S(1)}, bf16[1,8,2,32,128]{4,3,2,1,0:T(8,128)(2,1)S(1)}, u32[]{:S(2)}, u32[]{:S(2)}) collective-permute-start(bf16[1,8,2,32,128]{4,3,2,1,0:T(8,128)(2,1)S(1)} %collective-permute-done.8.refs_6_), channel_id=1, source_target_pairs={{32,34},{64,66},{96,98},{2,4},{34,36},{66,68},{98,100},{4,6},{36,3... | collective-permute-start | bytes 393224 | tf_op jit(solution)/shard_map/ppermute | solution.py:322
  115.0 4.2 %collective-permute-start.10 = (bf16[1,8,2,32,128]{4,3,2,1,0:T(8,128)(2,1)S(1)}, bf16[1,8,2,32,128]{4,3,2,1,0:T(8,128)(2,1)S(1)}, u32[]{:S(2)}, u32[]{:S(2)}) collective-permute-start(bf16[1,8,2,32,128]{4,3,2,1,0:T(8,128)(2,1)S(1)} %collective-permute-done.8.refs_6_), channel_id=1, source_target_pairs={{0,254},{32,158},{64,190},{96,222},{2,0},{34,32},{66,64},{98,96},{... | collective-permute-start | bytes 393224 | tf_op jit(solution)/shard_map/ppermute | solution.py:322
  119.2 2.0 %shard_map.49 = (f32[4,256,1]{2,1,0:T(8,128)S(1)}, f32[4,256,256]{2,1,0:T(8,128)S(1)}) custom-call(s32[8,128]{1,0:T(8,128)S(1)} %get-tuple-element.25.refs_0_, bf16[4,256,256]{2,1,0:T(8,128)(2,1)S(1)} %get-tuple-element.26.refs_1_, f32[4,256,1]{2,1,0:T(8,128)S(1)} %get-tuple-element.27.refs_2_, f32[4,256,256]{2,1,0:T(8,128)S(1)} %get-tuple-element.28.refs_3_, ...), custom_call_target="tpu_custom_call" | custom-call | flops 536870912 | bytes 2024288 | tf_op jit(solution)/shard_map/pallas_call | solution.py:217
  121.2 1.9 %shard_map.50 = (f32[4,256,1]{2,1,0:T(8,128)S(1)}, f32[4,256,256]{2,1,0:T(8,128)S(1)}) custom-call(s32[8,128]{1,0:T(8,128)S(1)} %get-tuple-element.25.refs_0_, bf16[4,256,256]{2,1,0:T(8,128)(2,1)S(1)} %get-tuple-element.26.refs_1_, f32[4,256,1]{2,1,0:T(8,128)S(1)} %get-tuple-element.31.refs_2_, f32[4,256,256]{2,1,0:T(8,128)S(1)} %get-tuple-element.32.refs_3_, ...), custom_call_target="tpu_custom_call" | custom-call | flops 402653184 | bytes 1893216 | tf_op jit(solution)/shard_map/pallas_call | solution.py:217
  123.1 0.0 collective-permute-done.7.refs_5_
  123.1 0.0 collective-permute-done.6.refs_4_
  123.1 2.9 %shard_map.51 = (f32[4,256,1]{2,1,0:T(8,128)S(1)}, f32[4,256,256]{2,1,0:T(8,128)S(1)}) custom-call(s32[8,128]{1,0:T(8,128)S(1)} %get-tuple-element.25.refs_0_, bf16[4,256,256]{2,1,0:T(8,128)(2,1)S(1)} %get-tuple-element.26.refs_1_, f32[4,256,1]{2,1,0:T(8,128)S(1)} %get-tuple-element.35.refs_2_, f32[4,256,256]{2,1,0:T(8,128)S(1)} %get-tuple-element.36.refs_3_, ...), custom_call_target="tpu_custom_call" | custom-call | flops 939524096 | bytes 2417504 | tf_op jit(solution)/shard_map/pallas_call | solution.py:217
  126.0 0.0 collective-permute-done.9.refs_4_
  126.0 0.0 collective-permute-done.10.refs_5_
  126.0 1.4 shard_map.52
  127.4 11.7 %all_to_all.16.in_ref = bf16[8,4,32,128]{3,2,1,0:T(8,128)(2,1)S(1)} all-to-all(bf16[8,4,32,128]{3,2,1,0:T(8,128)(2,1)S(1)} %shard_map.52), channel_id=1, replica_groups=mesh['x'=4,'zh'=2,'y'=4,'zl'=16,'c'=2] {'x','c'}, dimensions={0} | all-to-all | bytes 524288 | tf_op jit(solution)/shard_map/all_to_all | solution.py:331
  139.2 1.0 shard_map.53
  (5 shorter events, 0.1 us)
Async XLA Ops:
  11.2 28.5 %collective-permute-start = (bf16[1,8,2,32,128]{4,3,2,1,0:T(8,128)(2,1)S(1)}, bf16[1,8,2,32,128]{4,3,2,1,0:T(8,128)(2,1)S(1)}, u32[]{:S(2)}, u32[]{:S(2)}) collective-permute-start(bf16[1,8,2,32,128]{4,3,2,1,0:T(8,128)(2,1)S(1)} %bitcast.21), channel_id=1, source_target_pairs={{0,6},{32,38},{64,70},{96,102},{2,8},{34,40},{66,72},{98,104},{4,1... | collective-permute-start | bytes 393224 | tf_op jit(solution)/shard_map/ppermute | solution.py:322
  17.7 46.0 %collective-permute-start.3 = (bf16[1,8,2,32,128]{4,3,2,1,0:T(8,128)(2,1)S(1)}, bf16[1,8,2,32,128]{4,3,2,1,0:T(8,128)(2,1)S(1)}, u32[]{:S(2)}, u32[]{:S(2)}) collective-permute-start(bf16[1,8,2,32,128]{4,3,2,1,0:T(8,128)(2,1)S(1)} %bitcast.22), channel_id=1, source_target_pairs={{0,142},{32,174},{64,206},{96,238},{2,144},{34,176},{66,208},{98,2... | collective-permute-start | bytes 393224 | tf_op jit(solution)/shard_map/ppermute | solution.py:322
  39.7 24.1 %collective-permute-start.1 = (bf16[1,8,2,32,128]{4,3,2,1,0:T(8,128)(2,1)S(1)}, bf16[1,8,2,32,128]{4,3,2,1,0:T(8,128)(2,1)S(1)}, u32[]{:S(2)}, u32[]{:S(2)}) collective-permute-start(bf16[1,8,2,32,128]{4,3,2,1,0:T(8,128)(2,1)S(1)} %collective-permute-done.refs_3_), channel_id=1, source_target_pairs={{32,38},{64,70},{96,102},{34,40},{66,72},{98,104},{36,42},{68,74},... | collective-permute-start | bytes 393224 | tf_op jit(solution)/shard_map/ppermute | solution.py:322
  42.4 25.3 %collective-permute-start.2 = (bf16[2,8,2,32,128]{4,3,2,1,0:T(8,128)(2,1)S(1)}, bf16[2,8,2,32,128]{4,3,2,1,0:T(8,128)(2,1)S(1)}, u32[]{:S(2)}, u32[]{:S(2)}) collective-permute-start(bf16[2,8,2,32,128]{4,3,2,1,0:T(8,128)(2,1)S(1)} %pad_maximum_fusion.1), channel_id=1, source_target_pairs={{0,2},{32,34},{64,66},{96,98},{2,4},{34,36},{66,68},{98,100},{4,6}... | collective-permute-start | bytes 786440 | tf_op jit(solution)/shard_map/ppermute | solution.py:322
  63.8 12.1 %collective-permute-start.4 = (bf16[2,8,2,32,128]{4,3,2,1,0:T(8,128)(2,1)S(1)}, bf16[2,8,2,32,128]{4,3,2,1,0:T(8,128)(2,1)S(1)}, u32[]{:S(2)}, u32[]{:S(2)}) collective-permute-start(bf16[2,8,2,32,128]{4,3,2,1,0:T(8,128)(2,1)S(1)} %pad_maximum_fusion.2), channel_id=1, source_target_pairs={{32,34},{64,66},{96,98},{34,36},{66,68},{98,100},{36,38},{68,70},{... | collective-permute-start | bytes 786440 | tf_op jit(solution)/shard_map/ppermute | solution.py:322
  65.7 15.2 %collective-permute-start.5 = (bf16[1,8,2,32,128]{4,3,2,1,0:T(8,128)(2,1)S(1)}, bf16[1,8,2,32,128]{4,3,2,1,0:T(8,128)(2,1)S(1)}, u32[]{:S(2)}, u32[]{:S(2)}) collective-permute-start(bf16[1,8,2,32,128]{4,3,2,1,0:T(8,128)(2,1)S(1)} %collective-permute-done.3.refs_6_), channel_id=1, source_target_pairs={{0,250},{32,154},{64,186},{96,218},{2,252},{34,156},{66,188},{98,2... | collective-permute-start | bytes 393224 | tf_op jit(solution)/shard_map/ppermute | solution.py:322
  81.0 42.1 %collective-permute-start.6 = (bf16[4,8,2,32,128]{4,3,2,1,0:T(8,128)(2,1)S(1)}, bf16[4,8,2,32,128]{4,3,2,1,0:T(8,128)(2,1)S(1)}, u32[]{:S(2)}, u32[]{:S(2)}) collective-permute-start(bf16[4,8,2,32,128]{4,3,2,1,0:T(8,128)(2,1)S(1)} %pad_maximum_fusion), channel_id=1, source_target_pairs={{32,34},{64,66},{96,98},{2,4},{34,36},{66,68},{98,100},{4,6},{36,3... | collective-permute-start | bytes 1572872 | tf_op jit(solution)/shard_map/ppermute | solution.py:322
  84.8 11.5 %all-to-all-start = ((bf16[8,4,32,128]{3,2,1,0:T(8,128)(2,1)}), bf16[8,4,32,128]{3,2,1,0:T(8,128)(2,1)S(1)}, u32[]{:S(2)}, u32[]{:S(2)}) async-start(bf16[8,4,32,128]{3,2,1,0:T(8,128)(2,1)} %shard_map.46), calls=%async_computation | async-start | bytes 524288 | tf_op jit(solution)/shard_map/all_to_all | solution.py:315
  88.3 8.0 %copy-start = (s32[16]{0:T(128)S(1)}, s32[16]{0:T(128)}, u32[]{:S(2)}) copy-start(s32[16]{0:T(128)} %refs_0_.1) | copy-start | bytes 196
  88.3 34.8 %collective-permute-start.7 = (bf16[2,8,2,32,128]{4,3,2,1,0:T(8,128)(2,1)S(1)}, bf16[2,8,2,32,128]{4,3,2,1,0:T(8,128)(2,1)S(1)}, u32[]{:S(2)}, u32[]{:S(2)}) collective-permute-start(bf16[2,8,2,32,128]{4,3,2,1,0:T(8,128)(2,1)S(1)} %pad_maximum_fusion.3), channel_id=1, source_target_pairs={{0,254},{32,158},{64,190},{96,222},{34,32},{66,64},{98,96},{36,34}... | collective-permute-start | bytes 786440 | tf_op jit(solution)/shard_map/ppermute | solution.py:322
  94.3 16.9 %collective-permute-start.8 = (bf16[1,8,2,32,128]{4,3,2,1,0:T(8,128)(2,1)S(1)}, bf16[1,8,2,32,128]{4,3,2,1,0:T(8,128)(2,1)S(1)}, u32[]{:S(2)}, u32[]{:S(2)}) collective-permute-start(bf16[1,8,2,32,128]{4,3,2,1,0:T(8,128)(2,1)S(1)} %collective-permute-done.5.refs_5_), channel_id=1, source_target_pairs={{0,250},{32,154},{64,186},{96,218},{2,252},{34,156},{66,188},{98,2... | collective-permute-start | bytes 393224 | tf_op jit(solution)/shard_map/ppermute | solution.py:322
  111.2 14.8 %collective-permute-start.9 = (bf16[1,8,2,32,128]{4,3,2,1,0:T(8,128)(2,1)S(1)}, bf16[1,8,2,32,128]{4,3,2,1,0:T(8,128)(2,1)S(1)}, u32[]{:S(2)}, u32[]{:S(2)}) collective-permute-start(bf16[1,8,2,32,128]{4,3,2,1,0:T(8,128)(2,1)S(1)} %collective-permute-done.8.refs_6_), channel_id=1, source_target_pairs={{32,34},{64,66},{96,98},{2,4},{34,36},{66,68},{98,100},{4,6},{36,3... | collective-permute-start | bytes 393224 | tf_op jit(solution)/shard_map/ppermute | solution.py:322
  115.0 11.0 %collective-permute-start.10 = (bf16[1,8,2,32,128]{4,3,2,1,0:T(8,128)(2,1)S(1)}, bf16[1,8,2,32,128]{4,3,2,1,0:T(8,128)(2,1)S(1)}, u32[]{:S(2)}, u32[]{:S(2)}) collective-permute-start(bf16[1,8,2,32,128]{4,3,2,1,0:T(8,128)(2,1)S(1)} %collective-permute-done.8.refs_6_), channel_id=1, source_target_pairs={{0,254},{32,158},{64,190},{96,222},{2,0},{34,32},{66,64},{98,96},{... | collective-permute-start | bytes 393224 | tf_op jit(solution)/shard_map/ppermute | solution.py:322
